TPU v7x, 256 devices: a whole 4x4x8 slice. The times are simulated.
256 devices in a mesh: rep: 1, r: 32 (over y, z), s: 8 (over x, core).
Axes of the slice: x: 4, y: 4, z: 8, core: 2. Of those that a mesh axis runs over, the one named last changes fastest.
Arguments:
- x: bfloat16 [256, 2048, 896], P(('rep', 'r', 's'))
- dy: bfloat16 [256, 2048, 896], P(('rep', 'r', 's'))
- w_gate: bfloat16 [2, 896, 2304], P(None, 's')
- w_up: bfloat16 [2, 896, 2304], P(None, 's')
- w_down: bfloat16 [2, 2304, 896], P(None, 's')
Outputs:
- output 1: bfloat16 [256, 2048, 896], P(('rep', 'r', 's'))
- output 2: bfloat16 [2, 896, 2304], P('rep', 's')
- output 3: bfloat16 [2, 896, 2304], P('rep', 's')
- output 4: bfloat16 [2, 2304, 896], P('rep', 's')
All inputs are finite; a program needn't handle non-finite values.
Results may differ from a plain program's by a relative error of at most 0.018.
Values are sent between devices in bfloat16 or wider.
A program may use at most 768 MiB of HBM per device.

v0:
```python
import jax
import jax.numpy as jnp
from jax import lax
from jax.sharding import PartitionSpec as P

NAMES = ("w_gate", "w_up", "w_down")


def matmul(a, w):
    return jnp.dot(a, w, preferred_element_type=jnp.float32).astype(jnp.bfloat16)


def normed(h):
    wide = h.astype(jnp.float32)
    scale = lax.rsqrt(jnp.mean(wide**2, -1, keepdims=True) + 1e-6)
    return (wide * scale).astype(jnp.bfloat16)


def layer(h, w):
    a = normed(h)
    gate = jnp.dot(a, w["w_gate"], preferred_element_type=jnp.float32)
    up = jnp.dot(a, w["w_up"], preferred_element_type=jnp.float32)
    return h + matmul((jax.nn.silu(gate) * up).astype(jnp.bfloat16), w["w_down"])


def solution(mesh):
    def fetched(weights, number):
        return {name: lax.all_gather(w[number], "s", axis=0, tiled=True) for name, w in zip(NAMES, weights, strict=True)}

    def summed(term):
        return lax.psum(lax.psum_scatter(term, "s", scatter_dimension=0, tiled=True), "r")

    def step(x, dy, *weights):
        layers = weights[0].shape[0]
        h, inputs = x[0], []
        for number in range(layers):
            inputs.append(h)
            h = layer(h, fetched(weights, number))
        by_h, mine = dy[0], [None] * layers
        for number in reversed(range(layers)):
            _, back = jax.vjp(lambda w, h: layer(h, w), fetched(weights, number), inputs[number])
            by_w, by_h = back(by_h)
            mine[number] = [summed(by_w[name]) for name in NAMES]
        return (by_h[None], *(jnp.stack([mine[number][i] for number in range(layers)]) for i in range(3)))

    states, cut = P(("rep", "r", "s"), None, None), P(None, "s", None)
    return jax.shard_map(
        step,
        mesh=mesh,
        in_specs=(states, states) + (cut,) * 3,
        out_specs=(states,) + (P("rep", "s", None),) * 3,
        check_vma=False,
    )
```

profile of v0, /device:TPU:2, one launch (start us, length us, event | category | flops | bytes accessed | tf_op | source)
XLA Modules:
  0.0 733.0 jit_solution(3574536499863256245)
XLA Ops:
  7.2 2.2 fusion.68
  9.5 0.0 all-gather.15.cloned.1.call-start
  9.5 2.2 fusion.69
  11.8 0.0 all-gather.17.cloned.1.call-start
  11.8 2.3 fusion.70
  14.2 0.5 all-gather.23.cloned.1.call-update
  14.8 0.5 all-gather.21.cloned.1.call-update
  15.4 0.5 all-gather.19.cloned.1.call-update
  16.0 6.1 copy.10
  22.0 2.8 fusion.15
  24.8 0.6 copy-done.5
  25.4 6.2 copy.9
  31.6 14.8 %all-gather.13.cloned.1.call-done = bf16[1,896,2304]{2,1,0:T(8,128)(2,1)} async-done(((bf16[1,112,2304]{2,1,0:T(8,128)(2,1)}), bf16[1,896,2304]{2,1,0:T(8,128)(2,1)}) %all-gather.13.cloned.1.call-update) | async-done | bytes 4128784 | tf_op jit(solution)/shard_map/all_gather | solution.py:28
  46.4 16.6 %fusion.40 = f32[2048,2304]{1,0:T(8,128)} fusion(bf16[1,896,2304]{2,1,0:T(8,128)(2,1)} %all-gather.13.cloned.1.call-done, bf16[1,2048,896]{1,2,0:T(8,128)(2,1)} %copy.10, f32[2048]{0:T(1024)S(1)} %fusion.61), kind=kOutput, calls=%fused_computation.65 | convolution fusion | flops 8461221888 | bytes 26681344 | tf_op jit(solution)/shard_map/dot_general | solution.py:21
  63.0 19.3 %all-gather.15.cloned.1.call-done = bf16[1,896,2304]{2,1,0:T(8,128)(2,1)} async-done(((bf16[1,112,2304]{2,1,0:T(8,128)(2,1)}), bf16[1,896,2304]{2,1,0:T(8,128)(2,1)}) %all-gather.15.cloned.1.call-update) | async-done | bytes 4128784 | tf_op jit(solution)/shard_map/all_gather | solution.py:28
  82.3 23.2 %multiply_convert_fusion.1 = (bf16[2048,2304]{1,0:T(8,128)(2,1)}, f32[2048,2304]{1,0:T(8,128)}) fusion(f32[2048,2304]{1,0:T(8,128)} %fusion.40, bf16[1,896,2304]{2,1,0:T(8,128)(2,1)} %all-gather.15.cloned.1.call-done, bf16[1,2048,896]{1,2,0:T(8,128)(2,1)} %copy.10, f32[2048]{0:T(1024)S(1)} %fusion.61), kind=kOutput, calls=%fused_computation.13 | convolution fusion | flops 8489533440 | bytes 54992896 | tf_op jit(solution)/shard_map/dot_general | solution.py:22
  105.5 12.7 %all-gather.17.cloned.1.call-done = bf16[1,2304,896]{2,1,0:T(8,128)(2,1)} async-done(((bf16[1,288,896]{2,1,0:T(8,128)(2,1)}), bf16[1,2304,896]{2,1,0:T(8,128)(2,1)}) %all-gather.17.cloned.1.call-update) | async-done | bytes 4128784 | tf_op jit(solution)/shard_map/all_gather | solution.py:28
  118.2 14.9 %fusion.18 = (f32[2048]{0:T(1024)S(1)}, bf16[2048,896]{0,1:T(8,128)(2,1)}) fusion(bf16[2048,2304]{1,0:T(8,128)(2,1)} %get-tuple-element.20, bf16[1,2304,896]{2,1,0:T(8,128)(2,1)} %all-gather.17.cloned.1.call-done, bf16[1,2048,896]{1,2,0:T(8,128)(2,1)} %copy.10), kind=kOutput, calls=%fused_computation.40 | convolution fusion | flops 8464889856 | bytes 20914176 | tf_op jit(solution)/shard_map/dot_general | solution.py:10
  133.1 21.5 %all-gather.23.cloned.1.call-done = bf16[1,896,2304]{2,1,0:T(8,128)(2,1)} async-done(((bf16[1,112,2304]{2,1,0:T(8,128)(2,1)}), bf16[1,896,2304]{2,1,0:T(8,128)(2,1)}) %all-gather.23.cloned.1.call-update) | async-done | bytes 4128784 | tf_op jit(solution)/shard_map/all_gather | solution.py:28
  154.6 16.7 %fusion.24 = f32[2048,2304]{1,0:T(8,128)} fusion(bf16[1,896,2304]{2,1,0:T(8,128)(2,1)} %all-gather.23.cloned.1.call-done, bf16[2048,896]{0,1:T(8,128)(2,1)} %get-tuple-element.23, f32[2048]{0:T(1024)S(1)} %fusion.62), kind=kOutput, calls=%fused_computation.49 | convolution fusion | flops 8461221888 | bytes 26681344 | tf_op jit(solution)/shard_map/jvp()/dot_general | solution.py:22
  171.3 19.0 %all-gather.21.cloned.1.call-done = bf16[1,2304,896]{2,1,0:T(8,128)(2,1)} async-done(((bf16[1,288,896]{2,1,0:T(8,128)(2,1)}), bf16[1,2304,896]{2,1,0:T(8,128)(2,1)}) %all-gather.21.cloned.1.call-update) | async-done | bytes 4128784 | tf_op jit(solution)/shard_map/all_gather | solution.py:28
  190.3 15.0 %convolution_convert_fusion.1 = bf16[2048,2304]{1,0:T(8,128)(2,1)} fusion(bf16[1,2304,896]{2,1,0:T(8,128)(2,1)} %all-gather.21.cloned.1.call-done, bf16[1,2048,896]{2,1,0:T(8,128)(2,1)} %param.6), kind=kOutput, calls=%fused_computation.29 | convolution fusion | flops 8460435456 | bytes 17235968 | tf_op jit(solution)/shard_map/transpose(jvp())/dot_general | solution.py:10
  205.4 21.3 %all-gather.19.cloned.1.call-done = bf16[1,896,2304]{2,1,0:T(8,128)(2,1)} async-done(((bf16[1,112,2304]{2,1,0:T(8,128)(2,1)}), bf16[1,896,2304]{2,1,0:T(8,128)(2,1)}) %all-gather.19.cloned.1.call-update) | async-done | bytes 4128784 | tf_op jit(solution)/shard_map/all_gather | solution.py:28
  226.7 31.7 %fusion.1 = (bf16[2048,2304]{1,0:T(8,128)(2,1)}, f32[2048,2304]{1,0:T(8,128)}) fusion(f32[2048,2304]{1,0:T(8,128)} %fusion.24, bf16[2048,2304]{1,0:T(8,128)(2,1)} %convolution_convert_fusion.1, bf16[1,896,2304]{2,1,0:T(8,128)(2,1)} %all-gather.19.cloned.1.call-done, bf16[2048,896]{0,1:T(8,128)(2,1)} %get-tuple-element.23, f32[2048]{0:T(1024)S(1)} %fusion.62), kind=kOutput, calls=%fused_computation.7 | convolution fusion | flops 8517844992 | bytes 64430080 | tf_op jit(solution)/shard_map/jvp()/dot_general | solution.py:21
  258.4 16.8 %fusion.7 = bf16[2048,896]{0,1:T(8,128)(2,1)} fusion(bf16[2048,2304]{1,0:T(8,128)(2,1)} %convolution_convert_fusion.1, bf16[1,896,2304]{2,1,0:T(8,128)(2,1)} %all-gather.23.cloned.1.call-done, f32[2048,2304]{1,0:T(8,128)} %get-tuple-element.25), kind=kOutput, calls=%fused_computation.17 | convolution fusion | flops 8484028416 | bytes 36110336 | tf_op jit(solution)/shard_map/transpose(jvp())/dot_general | solution.py:22
  275.2 13.8 %fusion.20 = (f32[2048]{0:T(1024)S(1)}, bf16[2048,896]{0,1:T(8,128)(2,1)S(1)}) fusion(bf16[2048,896]{0,1:T(8,128)(2,1)S(1)} %copy-done.4, bf16[2048,896]{0,1:T(8,128)(2,1)} %fusion.7, bf16[2048,2304]{1,0:T(8,128)(2,1)} %get-tuple-element.24, bf16[1,896,2304]{2,1,0:T(8,128)(2,1)} %all-gather.19.cloned.1.call-done), kind=kOutput, calls=%fused_computation.42 | convolution fusion | flops 8464889856 | bytes 24584192 | tf_op jit(solution)/shard_map/transpose(jvp())/dot_general | solution.py:21
  289.0 2.7 fusion.44
  291.8 1.8 copy-done.2
  293.5 13.9 %convolution_convert_fusion.2 = bf16[2304,896]{1,0:T(8,128)(2,1)} fusion(bf16[2048,2304]{1,0:T(8,128)(2,1)} %get-tuple-element.20, bf16[2048,896]{0,1:T(8,128)(2,1)S(1)} %fusion.44), kind=kOutput, calls=%fused_computation.46 | convolution fusion | flops 8457781248 | bytes 17235968 | tf_op jit(solution)/shard_map/transpose(jvp())/dot_general | solution.py:10
  307.6 19.5 %fusion.21 = bf16[2304,896]{1,0:T(8,128)(2,1)} fusion(f32[2048,2304]{1,0:T(8,128)} %fusion.24, bf16[1,2048,896]{2,1,0:T(8,128)(2,1)} %param.6, f32[2048,2304]{1,0:T(8,128)} %get-tuple-element.25), kind=kOutput, calls=%fused_computation.43 | convolution fusion | flops 8486092800 | bytes 45547520 | tf_op jit(solution)/shard_map/transpose(jvp())/dot_general | solution.py:10
  327.1 0.0 reduce-scatter.11.cloned.1.call-start
  327.2 31.2 %fusion.3 = (bf16[2048,2304]{1,0:T(8,128)(2,1)}, bf16[2048,2304]{1,0:T(8,128)(2,1)}) fusion(f32[2048,2304]{1,0:T(8,128)} %fusion.40, f32[2048,2304]{1,0:T(8,128)} %get-tuple-element.21, bf16[2048,896]{0,1:T(8,128)(2,1)} %copy-done.2, bf16[1,2304,896]{2,1,0:T(8,128)(2,1)} %all-gather.17.cloned.1.call-done), kind=kOutput, calls=%fused_computation.9 | convolution fusion | flops 8517058560 | bytes 64421888 | tf_op jit(solution)/shard_map/transpose(jvp())/dot_general | solution.py:10
  358.4 18.0 %fusion.22 = bf16[896,2304]{1,0:T(8,128)(2,1)} fusion(bf16[2048,2304]{1,0:T(8,128)(2,1)} %get-tuple-element.29, bf16[1,2048,896]{1,2,0:T(8,128)(2,1)} %copy.10, f32[2048]{0:T(1024)S(1)} %copy-done.8, f32[2048,2304]{1,0:T(8,128)} %fusion.40), kind=kOutput, calls=%fused_computation.44 | convolution fusion | flops 8491597824 | bytes 36118528 | tf_op jit(solution)/shard_map/transpose(jvp())/dot_general | solution.py:22
  376.5 18.2 %fusion.23 = bf16[896,2304]{1,0:T(8,128)(2,1)} fusion(bf16[2048,2304]{1,0:T(8,128)(2,1)} %convolution_convert_fusion.1, bf16[2048,896]{0,1:T(8,128)(2,1)} %get-tuple-element.23, f32[2048]{0:T(1024)S(1)} %fusion.62, f32[2048,2304]{1,0:T(8,128)} %get-tuple-element.25), kind=kOutput, calls=%fused_computation.45 | convolution fusion | flops 8491597824 | bytes 36118528 | tf_op jit(solution)/shard_map/transpose(jvp())/dot_general | solution.py:22
  394.8 14.5 %convolution_convert_fusion.3 = bf16[896,2304]{1,0:T(8,128)(2,1)} fusion(bf16[2048,2304]{1,0:T(8,128)(2,1)} %get-tuple-element.24, bf16[2048,896]{0,1:T(8,128)(2,1)} %get-tuple-element.23, f32[2048]{0:T(1024)S(1)} %fusion.62), kind=kOutput, calls=%fused_computation.47 | convolution fusion | flops 8461221888 | bytes 17244160 | tf_op jit(solution)/shard_map/transpose(jvp())/dot_general | solution.py:21
  409.3 0.0 reduce-scatter.7.cloned.1.call-start
  409.4 14.5 %convolution_convert_fusion.4 = bf16[896,2304]{1,0:T(8,128)(2,1)} fusion(bf16[2048,2304]{1,0:T(8,128)(2,1)} %get-tuple-element.28, bf16[1,2048,896]{1,2,0:T(8,128)(2,1)} %copy.10, f32[2048]{0:T(1024)S(1)} %copy-done.8), kind=kOutput, calls=%fused_computation.48 | convolution fusion | flops 8461221888 | bytes 17244160 | tf_op jit(solution)/shard_map/transpose(jvp())/dot_general | solution.py:21
  423.9 0.0 all-reduce.3.cloned.1.call-start
  424.0 16.9 %fusion.9 = bf16[2048,896]{0,1:T(8,128)(2,1)} fusion(bf16[2048,2304]{1,0:T(8,128)(2,1)} %get-tuple-element.29, bf16[1,896,2304]{2,1,0:T(8,128)(2,1)} %all-gather.15.cloned.1.call-done, f32[2048,2304]{1,0:T(8,128)} %fusion.40), kind=kOutput, calls=%fused_computation.19 | convolution fusion | flops 8484028416 | bytes 36110336 | tf_op jit(solution)/shard_map/transpose(jvp())/dot_general | solution.py:22
  440.9 30.3 %reduce-scatter.13.cloned.1.call-done = bf16[112,2304]{1,0:T(8,128)(2,1)} async-done(((bf16[896,2304]{1,0:T(8,128)(2,1)}), bf16[112,2304]{1,0:T(8,128)(2,1)}) %reduce-scatter.13.cloned.1.call-update) | async-done | bytes 516112 | tf_op jit(solution)/shard_map/reduce_scatter | solution.py:31
  471.2 41.9 %reduce-scatter.9.cloned.1.call-done = bf16[112,2304]{1,0:T(8,128)(2,1)} async-done(((bf16[896,2304]{1,0:T(8,128)(2,1)}), bf16[112,2304]{1,0:T(8,128)(2,1)}) %reduce-scatter.9.cloned.1.call-update) | async-done | bytes 516112 | tf_op jit(solution)/shard_map/reduce_scatter | solution.py:31
  513.1 41.7 %reduce-scatter.7.cloned.1.call-done = bf16[112,2304]{1,0:T(8,128)(2,1)} async-done(((bf16[896,2304]{1,0:T(8,128)(2,1)}), bf16[112,2304]{1,0:T(8,128)(2,1)}) %reduce-scatter.7.cloned.1.call-update) | async-done | bytes 516112 | tf_op jit(solution)/shard_map/reduce_scatter | solution.py:31
  554.9 14.5 %fusion.17 = (f32[2048]{0:T(1024)S(1)}, bf16[2048,896]{0,1:T(8,128)(2,1)S(1)}) fusion(bf16[1,2048,896]{1,2,0:T(8,128)(2,1)} %copy.10, bf16[2048,896]{0,1:T(8,128)(2,1)} %fusion.9, bf16[2048,2304]{1,0:T(8,128)(2,1)} %get-tuple-element.28, bf16[1,896,2304]{2,1,0:T(8,128)(2,1)} %all-gather.13.cloned.1.call-done), kind=kOutput, calls=%fused_computation.39 | convolution fusion | flops 8464889856 | bytes 24584192 | tf_op jit(solution)/shard_map/transpose(jvp())/dot_general | solution.py:21
  569.5 4.5 fusion.43
  574.0 6.0 copy.11
  580.1 140.9 %all-reduce.3.cloned.1.call-done = (bf16[1,112,2304]{2,1,0:T(8,128)(2,1)}, bf16[1,112,2304]{2,1,0:T(8,128)(2,1)}, bf16[1,112,2304]{2,1,0:T(8,128)(2,1)}, bf16[1,...) async-done(((bf16[1,112,2304]{2,1,0:T(8,128)(2,1)}, bf16[1,112,2304]{2,1,0:T(8,128)(2,1)}, bf16[1,112,2304]{2,1,0:T(8,128)(2,1)}, ...) | async-done | bytes 3096592 | tf_op jit(solution)/shard_map/psum | solution.py:31
  721.0 2.3 pad_maximum_fusion.2
  723.3 3.0 pad_maximum_fusion
  (41 shorter events, 0.6 us)
Async XLA Ops:
  7.2 39.2 %all-gather.13.cloned.1.call-start = ((), (), s32[]{:S(2)}) async-start(), calls=%async_computation.12 | async-start | bytes 4644864 | tf_op jit(solution)/shard_map/all_gather | solution.py:28
  9.5 72.9 %all-gather.15.cloned.1.call-start = ((), (), s32[]{:S(2)}) async-start(), calls=%async_computation.13 | async-start | bytes 4644864 | tf_op jit(solution)/shard_map/all_gather | solution.py:28
  11.8 106.5 %all-gather.17.cloned.1.call-start = ((), (), s32[]{:S(2)}) async-start(), calls=%async_computation.14 | async-start | bytes 4644864 | tf_op jit(solution)/shard_map/all_gather | solution.py:28
  14.2 140.4 %all-gather.23.cloned.1.call-start = ((), (), s32[]{:S(2)}) async-start(), calls=%async_computation.17 | async-start | bytes 4644864 | tf_op jit(solution)/shard_map/all_gather | solution.py:28
  14.8 175.6 %all-gather.21.cloned.1.call-start = ((), (), s32[]{:S(2)}) async-start(), calls=%async_computation.16 | async-start | bytes 4644864 | tf_op jit(solution)/shard_map/all_gather | solution.py:28
  15.3 211.3 %all-gather.19.cloned.1.call-start = ((), (), s32[]{:S(2)}) async-start(), calls=%async_computation.15 | async-start | bytes 4644864 | tf_op jit(solution)/shard_map/all_gather | solution.py:28
  15.9 424.9 %reduce-scatter.15.cloned.1.call-start = ((), (), s32[]{:S(2)}) async-start(), calls=%async_computation.10 | async-start | bytes 4644864 | tf_op jit(solution)/shard_map/reduce_scatter | solution.py:31
  24.8 0.6 copy-start.5
  25.4 56.9 %copy-start.7 = (f32[2048]{0:T(1024)}, f32[2048]{0:T(1024)S(1)}, u32[]{:S(2)}) copy-start(f32[2048]{0:T(1024)S(1)} %fusion.61) | copy-start | bytes 24580
  258.4 16.8 %copy-start.4 = (bf16[2048,896]{0,1:T(8,128)(2,1)S(1)}, bf16[2048,896]{0,1:T(8,128)(2,1)}, u32[]{:S(2)}) copy-start(bf16[2048,896]{0,1:T(8,128)(2,1)} %get-tuple-element.23) | copy-start | bytes 11010052
  275.2 13.8 %copy-start.1 = (bf16[1,2048,896]{1,2,0:T(8,128)(2,1)S(1)}, bf16[1,2048,896]{1,2,0:T(8,128)(2,1)}, u32[]{:S(2)}) copy-start(bf16[1,2048,896]{1,2,0:T(8,128)(2,1)} %copy.9) | copy-start | bytes 11010052
  291.7 1.8 copy-start.2
  307.5 133.4 %reduce-scatter.17.cloned.1.call-start = ((), (), s32[]{:S(2)}) async-start(), calls=%async_computation.11 | async-start | bytes 4644864 | tf_op jit(solution)/shard_map/reduce_scatter | solution.py:31
  327.1 113.8 %reduce-scatter.11.cloned.1.call-start = ((), (), s32[]{:S(2)}) async-start(), calls=%async_computation.8 | async-start | bytes 4644864 | tf_op jit(solution)/shard_map/reduce_scatter | solution.py:31
  327.2 31.2 %copy-start.8 = (f32[2048]{0:T(1024)S(1)}, f32[2048]{0:T(1024)}, u32[]{:S(2)}) copy-start(f32[2048]{0:T(1024)} %copy-done.7) | copy-start | bytes 24580
  376.4 94.7 %reduce-scatter.13.cloned.1.call-start = ((), (), s32[]{:S(2)}) async-start(), calls=%async_computation.9 | async-start | bytes 4644864 | tf_op jit(solution)/shard_map/reduce_scatter | solution.py:31
  394.7 118.3 %reduce-scatter.9.cloned.1.call-start = ((), (), s32[]{:S(2)}) async-start(), calls=%async_computation.7 | async-start | bytes 4644864 | tf_op jit(solution)/shard_map/reduce_scatter | solution.py:31
  409.3 145.5 %reduce-scatter.7.cloned.1.call-start = ((), (), s32[]{:S(2)}) async-start(), calls=%async_computation.6 | async-start | bytes 4644864 | tf_op jit(solution)/shard_map/reduce_scatter | solution.py:31
  423.9 297.1 %all-reduce.3.cloned.1.call-start = ((), (), s32[]{:S(2)}) async-start(), calls=%async_computation.18 | async-start | bytes 6193152 | tf_op jit(solution)/shard_map/psum | solution.py:31
  554.9 14.6 %copy-start.6 = (f32[2048]{0:T(1024)S(1)}, f32[2048]{0:T(1024)}, u32[]{:S(2)}) copy-start(f32[2048]{0:T(1024)} %copy-done.5) | copy-start | bytes 24580
  554.9 14.6 %copy-start = (bf16[1,2048,896]{1,2,0:T(8,128)(2,1)S(1)}, bf16[1,2048,896]{1,2,0:T(8,128)(2,1)}, u32[]{:S(2)}) copy-start(bf16[1,2048,896]{1,2,0:T(8,128)(2,1)} %copy.10) | copy-start | bytes 11010052
  554.9 14.6 %copy-start.3 = (bf16[2048,896]{0,1:T(8,128)(2,1)S(1)}, bf16[2048,896]{0,1:T(8,128)(2,1)}, u32[]{:S(2)}) copy-start(bf16[2048,896]{0,1:T(8,128)(2,1)} %copy-done.2) | copy-start | bytes 11010052
Sparse Core Ops, SparseCore 0:
  10.4 35.9 all-gather.12
  48.2 34.0 all-gather.14
  84.2 34.0 all-gather.16
  120.5 34.0 all-gather.22
  156.3 34.0 all-gather.20
  192.6 34.0 all-gather.18
  307.6 37.9 reduce-scatter.14
  348.2 39.2 reduce-scatter.16
  390.1 39.2 reduce-scatter.10
  431.8 39.2 reduce-scatter.12
  473.8 39.2 reduce-scatter.8
  515.5 39.2 reduce-scatter.6
  559.1 161.8 all-reduce.2
where the time goes:
time: 739 us; the launch traced here: 733 us
  waiting for transfers between devices  365 us (49%)
  matrix products  310 us (42%)
  local copies, waits for them, and re-layouts  27.5 us (4%)
  other arithmetic  15.3 us (2%)
  between operations  14.3 us (2%)
    psum x1, waiting for transfers between devices, summed(): lax.psum(lax.psum_scatter(term, 's', scatter_dimension=0, tiled=True), 'r')  141 us
    reduce_scatter x6, waiting for transfers between devices, summed(): lax.psum_scatter(term, 's', scatter_dimension=0, tiled=True)  114 us
    dot_general x6, matrix products, layer(): up = jnp.dot(a, w['w_up'], preferred_element_type=jnp.float32)  110 us
    all_gather x6, waiting for transfers between devices, fetched(): lax.all_gather(w[number], 's', axis=0, tiled=True)  109 us
    dot_general x6, matrix products, layer(): gate = jnp.dot(a, w['w_gate'], preferred_element_type=jnp.float32)  106 us
    dot_general x5, matrix products, matmul(): jnp.dot(a, w, preferred_element_type=jnp.float32).astype(jnp.bfloat16)  94.6 us
    unnamed x21, local copies, waits for them, and re-layouts  20.7 us
  transfers between devices with their start and end apart: 13, of which 10 were waited for; matrix products, arithmetic and copies ran while one was open for 36% of the time, Pallas kernels for 0%

commit v1 on v0

v1 whole, which is shorter than its diff:
```python
import functools

import jax
import jax.numpy as jnp
from jax import lax
from jax.experimental import pallas as pl
from jax.experimental.pallas import tpu as pltpu
from jax.sharding import PartitionSpec as P

MESH = pl.DeviceIdType.MESH
f32, bf16 = jnp.float32, jnp.bfloat16

T, D, F, C = 2048, 896, 2304, 256
LAYERS, CHUNKS = 2, F // C
NX, NY, NZ, NS = 4, 4, 8, 8
RG, RD = D // NS, F // NS
PART = 42 * 16
PADDED = 44 * 16
QY, QZ = PADDED // NY, 32
TM = 512
TL = 256
NT = T // TL
PERIOD = CHUNKS + NT
LB, LC, LD, LE, LF = 1, 3, 4, 5, 6


def dot(a, b, ca=1, cb=0):
    return lax.dot_general(a, b, (((ca,), (cb,)), ((), ())), preferred_element_type=f32)


def normed(wide):
    scale = lax.rsqrt(jnp.mean(wide * wide, -1, keepdims=True) + 1e-6)
    return (wide * scale).astype(bf16)


def pack_kernel(wg, wu, wd, own):
    def gate_up(step, _):
        layer, i = step // 7, step % 7
        rows = pl.ds(pl.multiple_of(i * 16, 16), 16)
        for k, w in enumerate((wg, wu)):
            strip = w[layer, rows, :]
            for c in range(CHUNKS):
                for j in range(2):
                    parts = [strip[:, (9 * s + c) * 32 : (9 * s + c) * 32 + 32] for s in range(4 * j, 4 * j + 4)]
                    at = pl.ds(pl.multiple_of((k * 14 + j + i * 2) * 16, 16), 16)
                    own[layer * CHUNKS + c, at, :] = jnp.concatenate(parts, axis=1)
        return 0

    lax.fori_loop(0, 7 * LAYERS, gate_up, 0)

    def down(step, _):
        layer, c = step // CHUNKS, step % CHUNKS
        for i in range(2):
            strip = wd[layer, pl.ds(pl.multiple_of(c * 32 + i * 16, 16), 16), :]
            for j in range(7):
                own[step, pl.ds((28 + i * 7 + j) * 16, 16), :] = strip[:, j * 128 : j * 128 + 128]
        return 0

    lax.fori_loop(0, LAYERS * CHUNKS, down, 0)


def unpack_kernel(sums, og, ou, od):
    def gate_up(step, _):
        layer, i = step // 7, step % 7
        rows = pl.ds(pl.multiple_of(i * 16, 16), 16)
        for k, out in enumerate((og, ou)):
            for lane in range(18):
                parts = []
                for q in range(4 * lane, 4 * lane + 4):
                    s, c = q // 9, q % 9
                    at = pl.ds(pl.multiple_of((k * 14 + s // 4 + i * 2) * 16, 16), 16)
                    tile = sums[layer * CHUNKS + c, at, :]
                    parts.append(tile[:, s % 4 * 32 : s % 4 * 32 + 32])
                out[layer, rows, pl.ds(lane * 128, 128)] = jnp.concatenate(parts, axis=1)
        return 0

    lax.fori_loop(0, 7 * LAYERS, gate_up, 0)

    def down(step, _):
        layer, c = step // CHUNKS, step % CHUNKS
        for i in range(2):
            for j in range(7):
                od[layer, pl.ds(pl.multiple_of(c * 32 + i * 16, 16), 16), pl.ds(j * 128, 128)] = sums[
                    step, pl.ds((28 + i * 7 + j) * 16, 16), :
                ]
        return 0

    lax.fori_loop(0, LAYERS * CHUNKS, down, 0)


def kernel(
    own, x_in, dy_in,
    got, sums, dx_out,
    hx, dh, a, a_t, dh_t, wg, wu, wd, hid, dg, du, flat, xt,
    term, pair, x_out, x_got, y_out, y_got, z_out, z_got, z_sum, y_sum,
    g_send, g1_recv, g2_recv, g3_recv, load_sem, io_sem, xt_sem,
    pair_send, pair_recv, x_send, x_recv, y_send, y_recv, z_send, z_recv, zs_send, zs_recv, ys_send, ys_recv,
):
    s, r = lax.axis_index("s"), lax.axis_index("r")
    x, core, y, z = s // 2, s % 2, r // NZ, r % NZ

    def at(dx=0, dc=0, dy=0, dz=0):
        there = (y + dy) % NY * NZ + (z + dz) % NZ
        return (0, there, (x + dx) % NX * 2 + (core + dc) % 2)

    def shard(dx):
        return (x + dx) % NX * 2 + core

    def send(src, dst, send_sem, recv_sem, to):
        pltpu.make_async_remote_copy(
            src_ref=src, dst_ref=dst, send_sem=send_sem, recv_sem=recv_sem, device_id=to, device_id_type=MESH
        ).start()

    def wait(ref, sem):
        pltpu.make_async_copy(ref, ref, sem).wait()

    def rows(start, n):
        return pl.ds(pl.multiple_of(start, 16), n)

    def cols(c):
        return pl.ds(pl.multiple_of(c * C, C), C)

    def loop(n, body):
        lax.fori_loop(0, n, lambda i, _: (body(i), 0)[1], 0)

    get_x = pltpu.make_async_copy(x_in.at[0], hx, io_sem.at[0])
    get_dy = pltpu.make_async_copy(dy_in.at[0], dh, io_sem.at[1])
    get_x.start()
    get_dy.start()

    peers = [dict(dc=1)]
    peers += [dict(dx=i) for i in (1, 2, 3)] + [dict(dy=i) for i in (1, 2, 3)] + [dict(dz=i) for i in range(1, NZ)]
    barrier = pltpu.get_barrier_semaphore()
    for p in peers:
        pl.semaphore_signal(barrier, inc=1, device_id=at(**p), device_id_type=MESH)
    pl.semaphore_wait(barrier, len(peers))

    by_y, by_z = rows(y * 80, 80), rows(320 + z % 4 * 80, 80)

    def gather_1(ch):
        for dx in (1, 2, 3):
            for part in (by_y, by_z, pl.ds(640, 32)):
                send(own.at[ch, part], got.at[ch, s, part], g_send.at[ch], g1_recv.at[ch], at(dx=dx))

    def gather_2(ch):
        wait(got.at[ch, 0, pl.ds(0, 576)], g1_recv.at[ch])
        for dx in (1, 2, 3):
            here = shard(dx)

            def on(part, **to):
                part = got.at[ch, here, part]
                send(part, part, g_send.at[ch], g2_recv.at[ch], at(**to))

            on(by_z, dz=1)
            on(by_z, dz=-1)
            if dx == 1:
                on(by_z, dz=2)
            if dx == 2:
                on(rows(320 + z % 4 * 80, 48), dz=2)
                on(rows(368 + z % 4 * 80, 32), dz=-2)
            if dx == 3:
                on(by_z, dz=-2)
            for dy in (1, 2, 3):
                on(by_y, dy=dy)

    def gather_3(ch):
        wait(got.at[ch, pl.ds(0, 3), pl.ds(0, 480)], g2_recv.at[ch])
        send(own.at[ch], got.at[ch, s], g_send.at[ch], g3_recv.at[ch], at(dc=1))
        for dx in (1, 2, 3):
            part = got.at[ch, shard(dx)]
            send(part, part, g_send.at[ch], g3_recv.at[ch], at(dc=1))

    def load(ch):
        pltpu.make_async_copy(own.at[ch], flat.at[s], load_sem).start()
        for d in range(1, NS):
            other = (s + d) % NS
            pltpu.make_async_copy(got.at[ch, other], flat.at[other], load_sem).start()

    def arrived(ch):
        wait(got.at[ch, pl.ds(0, 4)], g3_recv.at[ch])

    def unpack(c):
        wait(flat, load_sem)

        def one(p):
            for i in range(7):
                for j in range(2):
                    there = (rows(p * RG + i * 16, 16), pl.ds(pl.multiple_of(c * C + j * 128, 128), 128))
                    wg[there] = flat[p, pl.ds((i * 2 + j) * 16, 16), :]
                    wu[there] = flat[p, pl.ds((14 + i * 2 + j) * 16, 16), :]
            for i in range(2):
                for j in range(7):
                    wd[rows(c * C + p * 32 + i * 16, 16), pl.ds(j * 128, 128)] = flat[p, pl.ds((28 + i * 7 + j) * 16, 16), :]

        loop(NS, one)

    def pump(ch):
        n = LAYERS * CHUNKS

        @pl.when(ch + 3 < n)
        def _():
            gather_2(ch + 3)

        @pl.when(ch + 2 < n)
        def _():
            gather_3(ch + 2)

        @pl.when(ch + 1 < n)
        def _():
            arrived(ch + 1)
            load(ch + 1)

    def add(out, *terms):
        out[...] = functools.reduce(lambda p, q: p + q, [t[...].astype(f32) for t in terms]).astype(bf16)

    def in_blocks(n, fn):
        loop(n // 176, lambda b: fn(rows(b * 176, 176)))

    def step_a(v):
        slot = v % 2
        for dx in range(NX):
            there = (x + dx) % NX
            send(term.at[slot, there * 2 + 1 - core], pair.at[slot, there], pair_send.at[slot], pair_recv.at[slot], at(dc=1))

    def step_b(v):
        slot, xs, xr = v % 2, v % 2, v % 4
        wait(pair.at[slot], pair_recv.at[slot])
        wait(pair.at[slot], pair_send.at[slot])
        for dx in (1, 2, 3, 0):
            there = (x + dx) % NX

            def block(part):
                out = x_out.at[xs, dx - 1, part] if dx else x_got.at[xr, 3, part]
                add(out, term.at[slot, there * 2 + core, part], pair.at[slot, there, part])

            in_blocks(PADDED, block)
            if dx:
                send(x_out.at[xs, dx - 1], x_got.at[xr, dx - 1], x_send.at[xs], x_recv.at[xr], at(dx=dx))

    def step_c(v):
        xs, xr, slot = v % 2, v % 4, v % 2
        wait(x_got.at[xr, pl.ds(0, 3)], x_recv.at[xr])
        wait(x_out.at[xs], x_send.at[xs])
        for dy in (1, 2, 3, 0):
            part = rows((y + dy) % NY * QY, QY)
            out = y_out.at[slot, dy - 1] if dy else y_got.at[slot, 3]
            add(out, *(x_got.at[xr, k, part] for k in (3, 0, 1, 2)))
            if dy:
                send(y_out.at[slot, dy - 1], y_got.at[slot, dy - 1], y_send.at[slot], y_recv.at[slot], at(dy=dy))

    def step_d(v):
        slot = v % 2
        wait(y_got.at[slot, pl.ds(0, 3)], y_recv.at[slot])
        wait(y_out.at[slot], y_send.at[slot])
        add(z_out.at[slot, pl.ds(0, QY)], *(y_got.at[slot, k] for k in (3, 0, 1, 2)))
        for dz in range(1, NZ):
            part = rows((z + dz) % NZ * QZ, QZ)
            send(z_out.at[slot, part], z_got.at[slot, dz - 1], z_send.at[slot], z_recv.at[slot], at(dz=dz))

    def step_e(v):
        slot = v % 2
        wait(z_got.at[slot], z_recv.at[slot])
        wait(z_got.at[slot], z_send.at[slot])
        mine = rows(z * QZ, QZ)
        add(z_sum.at[slot, mine], z_out.at[slot, mine], *(z_got.at[slot, k] for k in range(NZ - 1)))
        for dz in range(1, NZ):
            send(z_sum.at[slot, mine], z_sum.at[slot, mine], zs_send.at[slot], zs_recv.at[slot], at(dz=dz))

    def step_f(v):
        slot, ch = v % 2, chunk_of(v)
        wait(z_sum.at[slot, pl.ds(0, QZ * (NZ - 1))], zs_recv.at[slot])
        wait(z_sum.at[slot, pl.ds(0, QZ * (NZ - 1))], zs_send.at[slot])
        mine = rows(y * QY, QY)
        y_sum[ch] = z_sum[slot, pl.ds(0, QY), :]
        pltpu.make_async_copy(y_sum.at[ch], sums.at[ch, mine], ys_send.at[ch]).start()
        for dy in (1, 2, 3):
            send(y_sum.at[ch], sums.at[ch, mine], ys_send.at[ch], ys_recv.at[ch], at(dy=dy))

    def chunk_of(v):
        return (1 - v // PERIOD) * CHUNKS + v % PERIOD

    def tick(now):
        for lag, step in ((LF, step_f), (LE, step_e), (LD, step_d), (LC, step_c), (LB, step_b)):
            v = now - lag

            @pl.when((v >= 0) & (v < 2 * PERIOD) & (lax.rem(v + PERIOD, PERIOD) < CHUNKS))
            def _():
                step(v)

    loop(CHUNKS, gather_1)
    get_x.wait()

    def first_norm(m):
        part = rows(m * TL, TL)
        a[part, :] = normed(hx[part, :].astype(f32))

    loop(NT, first_norm)
    gather_2(0)
    gather_2(1)
    gather_3(0)
    gather_2(2)
    arrived(0)
    load(0)
    gather_3(1)

    def forward_half(c, half):
        for t in range(T // TM // 2):
            part = pl.ds(half * (T // 2) + t * TM, TM)
            gate = dot(a[part, :], wg[:, cols(c)])
            up = dot(a[part, :], wu[:, cols(c)])
            dg[part, cols(c)] = (jax.nn.silu(gate) * up).astype(bf16)

    def forward(c):
        unpack(c)
        gather_1(c + CHUNKS)
        forward_half(c, 0)
        pump(c)
        forward_half(c, 1)

    loop(CHUNKS, forward)
    get_dy.wait()

    def finish_forward(m):
        part = rows(m * TL, TL)
        lanes = pl.ds(pl.multiple_of(m * TL, TL), TL)
        out = dot(dg[part, :], wd[...]).astype(bf16)
        h = hx[part, :] + out
        hx[part, :] = h
        act = normed(h.astype(f32))
        a[part, :] = act
        a_t[:, lanes] = act.T
        dh_t[:, lanes] = dh[part, :].T

    loop(NT, finish_forward)

    def backward_half(c, half):
        for t in range(T // TM // 2):
            part = pl.ds(half * (T // 2) + t * TM, TM)
            gate = dot(a[part, :], wg[:, cols(c)])
            up = dot(a[part, :], wu[:, cols(c)])
            by_hid = dot(dh[part, :], wd[pl.ds(pl.multiple_of(c * C, C), C), :], 1, 1).astype(bf16).astype(f32)
            sig = jax.nn.sigmoid(gate)
            silu = gate * sig
            hid[part, :] = (silu * up).astype(bf16)
            dg[part, cols(c)] = (by_hid * up * (sig * (1 + gate * (1 - sig)))).astype(bf16)
            du[part, cols(c)] = (by_hid * silu).astype(bf16)

    def weight_grads(c, slot):
        for k, (left, right) in enumerate(((a_t, dg), (a_t, du), (dh_t, None))):
            out = dot(left[...], hid[...] if right is None else right[:, cols(c)])
            out = out.astype(bf16) if k < 2 else out.T.astype(bf16)
            up, wide = (7, 2) if k < 2 else (2, 7)
            for p in range(NS):
                for i in range(up):
                    for j in range(wide):
                        term[slot, p, pl.ds((k * 14 + i * wide + j) * 16, 16), :] = out[
                            (p * up + i) * 16 : (p * up + i) * 16 + 16, j * 128 : j * 128 + 128
                        ]

    for slot in range(2):
        for p in range(NS):
            term[slot, p, pl.ds(PART, PADDED - PART), :] = jnp.zeros((PADDED - PART, 128), bf16)
        z_out[slot, pl.ds(QY, NZ * QZ - QY), :] = jnp.zeros((NZ * QZ - QY, 128), bf16)

    def fetch(m, slot):
        return pltpu.make_async_copy(x_in.at[0, rows(m * TL, TL)], xt.at[slot], xt_sem.at[slot])

    def backward(turn):
        def first(c):
            v = turn * PERIOD + c
            ch = (1 - turn) * CHUNKS + c
            unpack(c)
            backward_half(c, 0)

            @pl.when(turn == 0)
            def _():
                pump(ch)

            @pl.when((turn == 0) & (c == CHUNKS - 1))
            def _():
                load(0)

            @pl.when((turn == 1) & (c < CHUNKS - 1))
            def _():
                load(c + 1)

            backward_half(c, 1)
            tick(v)
            weight_grads(c, v % 2)
            step_a(v)

        loop(CHUNKS, first)
        fetch(0, 0).start()

        def second(m):
            part = rows(m * TL, TL)
            lanes = pl.ds(pl.multiple_of(m * TL, TL), TL)
            fetch(m, m % 2).wait()

            @pl.when(m + 1 < NT)
            def _():
                fetch(m + 1, (m + 1) % 2).start()

            by_a = dot(dg[part, :], wg[...], 1, 1) + dot(du[part, :], wu[...], 1, 1)
            by_a = by_a.astype(bf16).astype(f32)
            wide = hx[part, :].astype(f32)
            scale = lax.rsqrt(jnp.mean(wide * wide, -1, keepdims=True) + 1e-6)
            along = jnp.mean(by_a * wide, -1, keepdims=True)
            by_h = (by_a * scale - wide * (scale * scale * scale * along)).astype(bf16)
            by_h = dh[part, :] + by_h
            dh[part, :] = by_h
            dh_t[:, lanes] = by_h.T
            h = xt[m % 2]
            hx[part, :] = h
            act = normed(h.astype(f32))
            a[part, :] = act
            a_t[:, lanes] = act.T
            tick(turn * PERIOD + CHUNKS + m)

        loop(NT, second)

    loop(2, backward)

    put_dx = pltpu.make_async_copy(dh, dx_out.at[0], io_sem.at[0])
    put_dx.start()

    def finish(ch):
        wait(sums.at[ch, pl.ds(0, 3 * QY)], ys_recv.at[ch])
        wait(sums.at[ch], ys_send.at[ch])
        wait(got.at[ch, pl.ds(0, 7)], g_send.at[ch])

    loop(LAYERS * CHUNKS, finish)
    put_dx.wait()


def solution(mesh):
    def step(x, dy, w_gate, w_up, w_down):
        anywhere = pl.BlockSpec(memory_space=pl.ANY)
        n = LAYERS * CHUNKS
        shape = jax.ShapeDtypeStruct
        own = pl.pallas_call(
            pack_kernel, out_shape=shape((n, PART, 128), bf16), compiler_params=pltpu.CompilerParams(vmem_limit_bytes=40 * 2**20)
        )(w_gate, w_up, w_down)
        vmem = lambda *dims, dtype=bf16: pltpu.VMEM(dims, dtype)
        dma = lambda *dims: pltpu.SemaphoreType.DMA(dims)
        _, sums, by_x = pl.pallas_call(
            kernel,
            out_shape=(shape((n, NS, PART, 128), bf16), shape((n, PADDED, 128), bf16), shape((1, T, D), bf16)),
            in_specs=[anywhere] * 3,
            out_specs=(anywhere,) * 3,
            scratch_shapes=[
                vmem(T, D), vmem(T, D), vmem(T, D), vmem(D, T), vmem(D, T),
                vmem(D, F), vmem(D, F), vmem(F, D), vmem(T, C), vmem(T, F), vmem(T, F),
                vmem(NS, PART, 128), vmem(2, TL, D),
                vmem(2, NS, PADDED, 128), vmem(2, NX, PADDED, 128), vmem(2, 3, PADDED, 128), vmem(4, 4, PADDED, 128),
                vmem(2, 3, QY, 128), vmem(2, 4, QY, 128), vmem(2, NZ * QZ, 128), vmem(2, NZ - 1, QZ, 128),
                vmem(2, NZ * QZ, 128), vmem(n, QY, 128),
                dma(n), dma(n), dma(n), dma(n), pltpu.SemaphoreType.DMA, dma(2), dma(2),
                dma(2), dma(2), dma(2), dma(4), dma(2), dma(2), dma(2), dma(2), dma(2), dma(2), dma(n), dma(n),
            ],
            compiler_params=pltpu.CompilerParams(collective_id=0, has_side_effects=True, vmem_limit_bytes=67043328),
        )(own, x, dy)
        grads = pl.pallas_call(
            unpack_kernel,
            out_shape=(shape((LAYERS, RG, F), bf16), shape((LAYERS, RG, F), bf16), shape((LAYERS, RD, D), bf16)),
            compiler_params=pltpu.CompilerParams(vmem_limit_bytes=40 * 2**20),
        )(sums)
        return (by_x, *grads)

    states, cut = P(("rep", "r", "s"), None, None), P(None, "s", None)
    return jax.shard_map(
        step,
        mesh=mesh,
        in_specs=(states, states) + (cut,) * 3,
        out_specs=(states,) + (P("rep", "s", None),) * 3,
        check_vma=False,
    )
```

time: 739 us -> 317 us (0.43)
  waiting for transfers between devices: 365 us -> 0 us
  matrix products: 310 us -> 0 us
  Pallas kernels: 0 us -> 303 us
  local copies, waits for them, and re-layouts: 27.5 us -> 11.4 us
  other arithmetic: 15.3 us -> 0 us
  between operations: 14.3 us -> 0.68 us
    dot_general x17 -> x0, matrix products: 310 us -> none  [the longest x6 110 us: layer(): up = jnp.dot(a, w['w_up'], preferred_element_type=jnp.float32)]
    pallas_call x0 -> x3, Pallas kernels: none -> 303 us  [the longest x1 295 us: step(): pl.pallas_call(kernel, out_shape=(shape((n, NS, PART, 128), bf16), shape(...]
    psum x1 -> x0, waiting for transfers between devices: 141 us -> none  [summed(): lax.psum(lax.psum_scatter(term, 's', scatter_dimension=0, tiled=True), 'r')]
    reduce_scatter x6 -> x0, waiting for transfers between devices: 114 us -> none  [summed(): lax.psum_scatter(term, 's', scatter_dimension=0, tiled=True)]
    all_gather x6 -> x0, waiting for transfers between devices: 109 us -> none  [fetched(): lax.all_gather(w[number], 's', axis=0, tiled=True)]
    unnamed x21 -> x11, local copies, waits for them, and re-layouts: 20.7 us -> 11.4 us
  transfers between devices with their start and end apart: 13 -> 0, of which waited for: 10 -> 0; matrix products, arithmetic and copies ran while one was open for 36% -> 0% of each run, Pallas kernels for 0% -> 0%
where the time goes in v1:
time: 317 us; the launch traced here: 315 us
  Pallas kernels  303 us (96%)
  local copies, waits for them, and re-layouts  11.4 us (4%)
    pallas_call x1, Pallas kernels, step(): pl.pallas_call(kernel, out_shape=(shape((n, NS, PART, 128), bf16), shape(...  295 us
    unnamed x11, local copies, waits for them, and re-layouts  11.4 us

profile of v1, /device:TPU:2, one launch (start us, length us, event | category | flops | bytes accessed | tf_op | source)
XLA Modules:
  0.0 314.6 jit_solution(5000193835882275801)
XLA Ops:
  0.6 0.0 copy-start.2
  0.6 1.2 copy-done.2
  1.9 0.0 copy-start.3
  1.9 1.2 copy-done.3
  3.1 0.0 copy-start.4
  3.1 1.2 copy-done.4
  4.3 2.9 shard_map.84.own
  7.2 0.0 copy-start
  7.2 1.6 copy-done
  8.8 295.2 %shard_map.85 = (bf16[18,8,672,128]{3,2,1,0:T(8,128)(2,1)}, bf16[18,704,128]{2,1,0:T(8,128)(2,1)}, bf16[1,2048,896]{2,1,0:T(8,128)(2,1)}) custom-call(bf16[18,672,128]{2,1,0:T(8,128)(2,1)} %copy-done, bf16[1,2048,896]{2,1,0:T(8,128)(2,1)} %x_in.1, bf16[1,2048,896]{2,1,0:T(8,128)(2,1)} %dy_in.1), custom_call_target="tpu_custom_call" | custom-call | tf_op jit(solution)/shard_map/pallas_call | solution.py:446
  304.0 0.0 copy-start.1
  304.0 1.9 copy-done.1
  305.9 4.5 %shard_map.86 = (bf16[2,112,2304]{2,1,0:T(8,128)(2,1)}, bf16[2,112,2304]{2,1,0:T(8,128)(2,1)}, bf16[2,288,896]{2,1,0:T(8,128)(2,1)}) custom-call(bf16[18,704,128]{2,1,0:T(8,128)(2,1)S(1)} %copy-done.1), custom_call_target="tpu_custom_call" | custom-call | tf_op jit(solution)/shard_map/pallas_call | solution.py:463
  310.4 4.2 %copy.10 = bf16[1,2048,896]{2,1,0:T(8,128)(2,1)} copy(bf16[1,2048,896]{2,1,0:T(8,128)(2,1)} %get-tuple-element.18) | data formatting | bytes 7340032
Async XLA Ops:
  0.6 1.2 copy-start.2
  1.9 1.2 copy-start.3
  3.1 1.2 copy-start.4
  7.2 1.7 copy-start
  304.0 1.9 copy-start.1

commit v2 on v0

v2 whole, which is shorter than its diff:
```python
import functools

import jax
import jax.numpy as jnp
from jax import lax
from jax.experimental import pallas as pl
from jax.experimental.pallas import tpu as pltpu
from jax.sharding import PartitionSpec as P

MESH = pl.DeviceIdType.MESH
f32, bf16 = jnp.float32, jnp.bfloat16

T, D, F, C = 2048, 896, 2304, 256
LAYERS, CHUNKS = 2, F // C
N = LAYERS * CHUNKS
NX, NY, NZ, NS = 4, 4, 8, 8
RG, RD = D // NS, F // NS
PART = 42 * 16
PADDED = 44 * 16
QY, QZ = PADDED // NY, 32
QA = 112
QB = QY - QA
TM = 512
TL = 256
NT = T // TL
PERIOD = CHUNKS + NT // 2
LB, LC, LD, LE, LF, LG = 1, 3, 5, 7, 9, 10


def dot(a, b, ca=1, cb=0):
    return lax.dot_general(a, b, (((ca,), (cb,)), ((), ())), preferred_element_type=f32)


def normed(wide):
    scale = lax.rsqrt(jnp.mean(wide * wide, -1, keepdims=True) + 1e-6)
    return (wide * scale).astype(bf16)


def mod(a, b):
    return a % b if isinstance(a, int) else lax.rem(a, b)


def div(a, b):
    return a // b if isinstance(a, int) else lax.div(a, b)


def in2(v):
    return mod(v, 2)


def in4(v):
    return mod(v, 4)


def rows(start, n):
    return pl.ds(pl.multiple_of(start, 16), n)


def cols(c):
    return pl.ds(pl.multiple_of(c * C, C), C)


def loop(n, body):
    lax.fori_loop(0, n, lambda i, _: (body(i), 0)[1], 0)


def wait(ref, sem):
    pltpu.make_async_copy(ref, ref, sem).wait()


def unpack_kernel(sums_in, dx_in, dx_out, og_out, ou_out, od_out, sums, dx, og, ou, od, in_sem, dx_sem, out_sem):
    for layer in (1, 0):
        half = pl.ds(layer * CHUNKS, CHUNKS)
        pltpu.make_async_copy(sums_in.at[half], sums.at[half], in_sem.at[layer]).start()
    moves = []
    for k in range(4):
        part = pl.ds(k * (T // 4), T // 4)
        pltpu.make_async_copy(dx_in.at[0, part], dx.at[part], dx_sem.at[k]).start()
        moves.append((dx_in.at[0, part], dx.at[part], dx_out.at[0, part], dx_sem.at[k]))
    for src, mid, dst, sem in moves:
        pltpu.make_async_copy(src, mid, sem).wait()
        pltpu.make_async_copy(mid, dst, sem).start()
    for layer in (1, 0):
        wait(sums.at[pl.ds(layer * CHUNKS, CHUNKS)], in_sem.at[layer])

        def gate_up(i):
            for k, out in enumerate((og, ou)):
                for lane in range(18):
                    parts = []
                    for q in range(4 * lane, 4 * lane + 4):
                        s, c = q // 9, q % 9
                        at = rows((k * 14 + s // 4 + i * 2) * 16, 16)
                        parts.append(sums[layer * CHUNKS + c, at, :][:, s % 4 * 32 : s % 4 * 32 + 32])
                    out[layer, rows(i * 16, 16), pl.ds(lane * 128, 128)] = jnp.concatenate(parts, axis=1)

        loop(7, gate_up)

        def down(c):
            for i in range(2):
                for j in range(7):
                    there = (layer, rows(c * 32 + i * 16, 16), pl.ds(j * 128, 128))
                    od[there] = sums[layer * CHUNKS + c, pl.ds((28 + i * 7 + j) * 16, 16), :]

        loop(CHUNKS, down)
        for k, (mid, out) in enumerate(((og, og_out), (ou, ou_out), (od, od_out))):
            pltpu.make_async_copy(mid.at[layer], out.at[layer], out_sem.at[layer * 3 + k]).start()
    for layer in (1, 0):
        for k, (mid, out) in enumerate(((og, og_out), (ou, ou_out), (od, od_out))):
            pltpu.make_async_copy(mid.at[layer], out.at[layer], out_sem.at[layer * 3 + k]).wait()
    for _, mid, dst, sem in moves:
        pltpu.make_async_copy(mid, dst, sem).wait()


def kernel(
    x_in, dy_in, wg_in, wu_in, wd_in,
    own, got, sums, dx_out, kept, kept_hid,
    hx, dh, a, a_t, dh_t, wg, wu, wd, hid, dg, du, keep, flat, xt,
    term, pair, both, x_got, y_got, a_out, b_out, a_got, b_got, z_out, z_got, z_sum, y_sum,
    w_sem, own_sem, fence_sem, g1_send, g_send, g1_recv, g2_recv, g3_recv, load_sem, io_sem, xt_sem, keep_sem, hid_sem,
    pair_send, pair_recv, x_send, x_recv, y_send, y_recv, a_send, a_recv, b_send, b_recv,
    z_send, z_recv, zs_send, zs_recv, ys_send, ys_recv,
):
    s, r = lax.axis_index("s"), lax.axis_index("r")
    x, core, y, z = div(s, 2), mod(s, 2), div(r, NZ), mod(r, NZ)

    def at(dx=0, dc=0, dy=0, dz=0):
        there = mod(y + dy, NY) * NZ + mod(z + dz, NZ)
        return (0, there, mod(x + dx, NX) * 2 + mod(core + dc, 2))

    def shard(dx):
        return mod(x + dx, NX) * 2 + core

    def send(src, dst, send_sem, recv_sem, to):
        pltpu.make_async_remote_copy(
            src_ref=src, dst_ref=dst, send_sem=send_sem, recv_sem=recv_sem, device_id=to, device_id_type=MESH
        ).start()

    def get_weights(layer):
        for k, w in enumerate((wg_in, wu_in)):
            there = du.at[pl.ds((layer * 2 + k) * RG, RG)]
            pltpu.make_async_copy(w.at[layer], there, w_sem.at[layer]).start()
        there = dh_t.at[pl.ds(layer * RD, RD), pl.ds(0, D)]
        pltpu.make_async_copy(wd_in.at[layer], there, w_sem.at[layer + 2]).start()

    get_weights(0)
    get_x = pltpu.make_async_copy(x_in.at[0], hx, io_sem.at[0])
    get_dy = pltpu.make_async_copy(dy_in.at[0], dh, io_sem.at[1])

    peers = [dict(dc=1)]
    peers += [dict(dx=i) for i in (1, 2, 3)] + [dict(dy=i) for i in (1, 2, 3)] + [dict(dz=i) for i in range(1, NZ)]
    barrier = pltpu.get_barrier_semaphore()
    for p in peers:
        pl.semaphore_signal(barrier, inc=1, device_id=at(**p), device_id_type=MESH)

    def staged(ch):
        return term.at[div(ch, NS), mod(ch, NS)] if ch < 2 * NS else pair.at[0, ch - 2 * NS]

    def pack(layer):
        wait(du.at[pl.ds(0, 2 * RG)], w_sem.at[layer])
        wait(dh_t.at[pl.ds(0, RD), pl.ds(0, D)], w_sem.at[layer + 2])

        def gate_up(i):
            for k in range(2):
                strip = du[rows((layer * 2 + k) * RG + i * 16, 16), :]
                for c in range(CHUNKS):
                    for j in range(2):
                        there = staged(layer * CHUNKS + c)
                        for q in range(4):
                            old = (9 * (4 * j + q) + c) * 32
                            there[rows((k * 14 + j + i * 2) * 16, 16), pl.ds(q * 32, 32)] = strip[:, old : old + 32]

        loop(7, gate_up)
        for c in range(CHUNKS):
            there = staged(layer * CHUNKS + c)
            for i in range(2):
                for j in range(7):
                    tile = dh_t[pl.ds(layer * RD + c * 32 + i * 16, 16), pl.ds(j * 128, 128)]
                    there[pl.ds((28 + i * 7 + j) * 16, 16), :] = tile
            pltpu.make_async_copy(there.at[pl.ds(0, PART)], own.at[layer * CHUNKS + c], own_sem).start()

    def packed():
        wait(own.at[pl.ds(0, CHUNKS)], own_sem)

    by_y, by_z = rows(y * 80, 80), rows(320 + mod(z, 4) * 80, 80)

    def gather_1(ch, part_of, sem):
        for dx in (1, 2, 3):
            for part in (by_y, by_z, pl.ds(640, 32)):
                send(part_of.at[part], got.at[ch, s, part], sem, g1_recv.at[ch], at(dx=dx))

    def gather_2(ch):
        wait(got.at[ch, 0, pl.ds(0, 576)], g1_recv.at[ch])
        for dx in (1, 2, 3):
            here = shard(dx)

            def on(part, **to):
                part = got.at[ch, here, part]
                send(part, part, g_send.at[ch], g2_recv.at[ch], at(**to))

            on(by_z, dz=1)
            on(by_z, dz=NZ - 1)
            if dx == 1:
                on(by_z, dz=2)
            if dx == 2:
                on(rows(320 + mod(z, 4) * 80, 48), dz=2)
                on(rows(368 + mod(z, 4) * 80, 32), dz=NZ - 2)
            if dx == 3:
                on(by_z, dz=NZ - 2)
            for dy in (1, 2, 3):
                on(by_y, dy=dy)

    def gather_3(ch):
        wait(got.at[ch, pl.ds(0, 3), pl.ds(0, 480)], g2_recv.at[ch])
        send(own.at[ch], got.at[ch, s], g_send.at[ch], g3_recv.at[ch], at(dc=1))
        for dx in (1, 2, 3):
            part = got.at[ch, shard(dx)]
            send(part, part, g_send.at[ch], g3_recv.at[ch], at(dc=1))

    def load(ch):
        pltpu.make_async_copy(own.at[ch], flat.at[s], load_sem).start()
        for d in range(1, NS):
            other = mod(s + d, NS)
            pltpu.make_async_copy(got.at[ch, other], flat.at[other], load_sem).start()

    def arrived(ch):
        wait(got.at[ch, pl.ds(0, 4)], g3_recv.at[ch])

    def loaded():
        wait(flat, load_sem)

    def unpack_one(c, p):
        for i in range(7):
            for j in range(2):
                there = (rows(p * RG + i * 16, 16), pl.ds(pl.multiple_of(c * C + j * 128, 128), 128))
                wg[there] = flat[p, pl.ds((i * 2 + j) * 16, 16), :]
                wu[there] = flat[p, pl.ds((14 + i * 2 + j) * 16, 16), :]
        for i in range(2):
            for j in range(7):
                wd[rows(p * 32 + i * 16, 16), pl.ds(j * 128, 128)] = flat[p, pl.ds((28 + i * 7 + j) * 16, 16), :]

    def unpack(c):
        loop(NS, lambda p: unpack_one(c, p))

    def pump(ch):
        pl.when(ch + 3 < N)(lambda: gather_2(ch + 3))
        pl.when(ch + 2 < N)(lambda: gather_3(ch + 2))

        @pl.when(ch + 1 < N)
        def _():
            arrived(ch + 1)
            load(ch + 1)

    def fence():
        pl.semaphore_signal(fence_sem, 1)
        pl.semaphore_wait(fence_sem, 1)

    def total(*terms):
        return functools.reduce(lambda p, q: p + q, [t.astype(f32) for t in terms]).astype(bf16)

    def step_a(v):
        slot = in2(v)
        for dx in range(NX):
            there = mod(x + dx, NX)
            send(term.at[slot, there * 2 + 1 - core], pair.at[slot, there], pair_send.at[slot], pair_recv.at[slot], at(dc=1))

    def wait_b(v):
        wait(pair.at[in2(v)], pair_recv.at[in2(v)])
        wait(pair.at[in2(v)], pair_send.at[in2(v)])

    def add_b(v, each):
        def one(k):
            i, part = div(k, NY), rows(mod(k, NY) * QY, QY)
            both[in2(v), i, mod(k, NY)] = total(term[in2(v), i * 2 + core, part, :], pair[in2(v), i, part, :])

        each(NX * NY, one)

    def send_b(v):
        for d in (1, 2, 3):
            src = both.at[in2(v), mod(x + d, NX), :, pl.ds(0, QA)]
            send(src, x_got.at[in4(v), d - 1], x_send.at[in2(v)], x_recv.at[in4(v)], at(dx=d))
            src = both.at[in2(v), :, mod(y + d, NY), pl.ds(QA, QB)]
            send(src, y_got.at[in4(v), d - 1], y_send.at[in2(v)], y_recv.at[in4(v)], at(dy=d))

    def wait_c(v):
        wait(x_got.at[in4(v)], x_recv.at[in4(v)])
        wait(y_got.at[in4(v)], y_recv.at[in4(v)])
        wait(x_got.at[in4(v)], x_send.at[in2(v)])
        wait(y_got.at[in4(v)], y_send.at[in2(v)])

    def add_c(v, each):
        for d in range(4):
            there = mod(y + d, NY)
            out = total(both[in2(v), x, there, pl.ds(0, QA), :], *(x_got[in4(v), k, there] for k in range(3)))
            if d:
                a_out[in2(v), d - 1] = out
            else:
                a_got[in4(v), 3] = out
            there = mod(x + d, NX)
            out = total(both[in2(v), there, y, pl.ds(QA, QB), :], *(y_got[in4(v), k, there] for k in range(3)))
            if d:
                b_out[in2(v), d - 1] = out
            else:
                b_got[in4(v), 3] = out

    def send_c(v):
        for d in (1, 2, 3):
            send(a_out.at[in2(v), d - 1], a_got.at[in4(v), d - 1], a_send.at[in4(v)], a_recv.at[in4(v)], at(dy=d))
            send(b_out.at[in2(v), d - 1], b_got.at[in4(v), d - 1], b_send.at[in4(v)], b_recv.at[in4(v)], at(dx=d))

    def wait_d(v):
        wait(a_out.at[in2(v)], a_recv.at[in4(v)])
        wait(b_out.at[in2(v)], b_recv.at[in4(v)])
        wait(a_out.at[in2(v)], a_send.at[in4(v)])
        wait(b_out.at[in2(v)], b_send.at[in4(v)])

    def add_d(v, each):
        z_out[in4(v), pl.ds(0, QA), :] = total(*(a_got[in4(v), k] for k in (3, 0, 1, 2)))
        z_out[in4(v), pl.ds(QA, QB), :] = total(*(b_got[in4(v), k] for k in (3, 0, 1, 2)))

    def send_d(v):
        for d in range(1, NZ):
            src = z_out.at[in4(v), rows(mod(z + d, NZ) * QZ, QZ)]
            send(src, z_got.at[in4(v), d - 1], z_send.at[in4(v)], z_recv.at[in4(v)], at(dz=d))

    def wait_e(v):
        wait(z_got.at[in4(v)], z_recv.at[in4(v)])
        wait(z_got.at[in4(v)], z_send.at[in4(v)])

    def add_e(v, each):
        mine = rows(z * QZ, QZ)
        z_sum[in4(v), mine, :] = total(z_out[in4(v), mine, :], *(z_got[in4(v), k] for k in range(NZ - 1)))

    def send_e(v):
        mine = z_sum.at[in4(v), rows(z * QZ, QZ)]
        for d in range(1, NZ):
            send(mine, mine, zs_send.at[in4(v)], zs_recv.at[in4(v)], at(dz=d))

    def wait_f(v):
        wait(z_sum.at[in4(v), pl.ds(0, QZ * (NZ - 1))], zs_recv.at[in4(v)])
        wait(z_sum.at[in4(v), pl.ds(0, QZ * (NZ - 1))], zs_send.at[in4(v)])

    def send_f(v):
        ch, mine = (1 - div(v, PERIOD)) * CHUNKS + mod(v, PERIOD), rows(y * QY, QY)
        y_sum[in2(v)] = z_sum[in4(v), pl.ds(0, QY), :]
        pltpu.make_async_copy(y_sum.at[in2(v)], sums.at[ch, mine], ys_send.at[in4(v)]).start()
        for d in (1, 2, 3):
            send(y_sum.at[in2(v)], sums.at[ch, mine], ys_send.at[in4(v)], ys_recv.at[ch], at(dy=d))

    def wait_g(v):
        wait(sums.at[0], ys_send.at[in4(v)])

    def send_g(v):
        pass

    steps = (
        (LG, wait_g, None, send_g),
        (LF, wait_f, None, send_f),
        (LE, wait_e, add_e, send_e),
        (LD, wait_d, add_d, send_d),
        (LC, wait_c, add_c, send_c),
        (LB, wait_b, add_b, send_b),
    )

    def real(v):
        return (v >= 0) & (v < 2 * PERIOD) & (lax.rem(v + PERIOD, PERIOD) < CHUNKS)

    def waits(now, steps=steps):
        for lag, first, _, _ in steps:
            pl.when(real(now - lag))(lambda: first(now - lag))

    def adds(now, steps=steps):
        for lag, _, add, _ in steps:
            if add:
                pl.when(real(now - lag))(lambda: add(now - lag, loop))

    def unrolled(n, body):
        for k in range(n):
            body(k)

    def sends(now):
        for lag, _, _, last in steps:
            pl.when(real(now - lag))(lambda: last(now - lag))

    def tick(now):
        waits(now)
        adds(now)
        sends(now)

    pack(0)
    get_x.start()
    get_weights(1)
    pl.semaphore_wait(barrier, len(peers))
    for ch in range(CHUNKS):
        gather_1(ch, staged(ch), g1_send.at[0])
    get_x.wait()

    def first_norm(m):
        part = rows(m * TL, TL)
        a[part, :] = normed(hx[part, :].astype(f32))

    loop(NT, first_norm)
    gather_2(0)
    gather_2(1)
    packed()
    pack(1)
    get_dy.start()
    gather_3(0)
    gather_2(2)
    packed()
    arrived(0)
    load(0)
    gather_3(1)

    def keeping(c, half):
        part = pl.ds(half * (T // 2), T // 2)
        return pltpu.make_async_copy(keep.at[:, part], kept.at[c, :, part], keep_sem.at[half])

    def forward_half(c, half):
        for t in range(T // TM // 2):
            part = pl.ds(half * (T // 2) + t * TM, TM)
            gate = dot(a[part, :], wg[:, cols(c)])
            up = dot(a[part, :], wu[:, cols(c)])
            sig = jax.nn.sigmoid(gate)
            silu = gate * sig
            dg[part, cols(c)] = (silu * up).astype(bf16)
            keep[0, part, :] = silu
            keep[1, part, :] = up * (sig * (1 + gate * (1 - sig)))

    def forward(c):
        loaded()
        unpack(c)
        gather_1(c + CHUNKS, own.at[c + CHUNKS], g1_send.at[1])
        pl.when(c >= 1)(lambda: keeping(c, 0).wait())
        du[pl.ds(0, D), cols(c)] = wd[...].T
        forward_half(c, 0)
        keeping(c, 0).start()
        pump(c)
        fence()
        pl.when(c >= 1)(lambda: keeping(c, 1).wait())
        forward_half(c, 1)
        keeping(c, 1).start()

    loop(CHUNKS, forward)
    get_dy.wait()

    loop(CHUNKS, lambda c: pltpu.make_async_copy(dg.at[:, cols(c)], kept_hid.at[c], hid_sem).start())

    def finish_forward(m):
        part = rows(m * TL, TL)
        lanes = pl.ds(pl.multiple_of(m * TL, TL), TL)
        out = dot(dg[part, :], du[pl.ds(0, D), :], 1, 1).astype(bf16)
        h = hx[part, :] + out
        hx[part, :] = h
        act = normed(h.astype(f32))
        a[part, :] = act
        a_t[:, lanes] = act.T
        dh_t[:, lanes] = dh[part, :].T

    loop(NT, finish_forward)
    keeping(0, 0).wait()
    keeping(0, 1).wait()
    wait(dg, hid_sem)

    def fetch_kept(c):
        return (
            pltpu.make_async_copy(kept.at[c], keep, keep_sem.at[0]),
            pltpu.make_async_copy(kept_hid.at[c], hid.at[in2(c)], hid_sem),
        )

    def by_hid(part):
        return dot(dh[part, :], wd[...], 1, 1).astype(bf16).astype(f32)

    def backward_half(c, half):
        for t in range(T // TM // 2):
            part = pl.ds(half * (T // 2) + t * TM, TM)
            gate = dot(a[part, :], wg[:, cols(c)])
            up = dot(a[part, :], wu[:, cols(c)])
            by = by_hid(part)
            sig = jax.nn.sigmoid(gate)
            silu = gate * sig
            hid[1, part, :] = (silu * up).astype(bf16)
            dg[part, cols(c)] = (by * (up * (sig * (1 + gate * (1 - sig))))).astype(bf16)
            du[part, cols(c)] = (by * silu).astype(bf16)

    def backward_kept(c):
        for t in range(T // TM):
            part = pl.ds(t * TM, TM)
            by = by_hid(part)
            dg[part, cols(c)] = (by * keep[1, part, :]).astype(bf16)
            du[part, cols(c)] = (by * keep[0, part, :]).astype(bf16)

    def weight_grads(c, slot, hid_slot):
        for k, (left, right) in enumerate(((a_t, dg), (a_t, du), (dh_t, None))):
            out = dot(left[...], hid[hid_slot] if right is None else right[:, cols(c)])
            out = out.astype(bf16) if k < 2 else out.T.astype(bf16)
            up, wide = (7, 2) if k < 2 else (2, 7)
            for p in range(NS):
                for i in range(up):
                    for j in range(wide):
                        term[slot, p, pl.ds((k * 14 + i * wide + j) * 16, 16), :] = out[
                            (p * up + i) * 16 : (p * up + i) * 16 + 16, j * 128 : j * 128 + 128
                        ]

    wait(got.at[pl.ds(0, CHUNKS), 0, pl.ds(0, 576)], g1_send.at[0])
    for slot in range(4):
        z_out[slot, pl.ds(QY, NZ * QZ - QY), :] = jnp.zeros((NZ * QZ - QY, 128), bf16)
    for slot in range(2):
        for p in range(NS):
            term[slot, p, pl.ds(PART, PADDED - PART), :] = jnp.zeros((PADDED - PART, 128), bf16)

    def gradients(turn, c, hid_slot):
        v = turn * PERIOD + c
        beside = steps[:-1] if turn else steps
        waits(v, beside)
        pl.when(c < CHUNKS - 1)(loaded)
        adds(v, steps[:-1])
        if not turn:
            add_b(v + 1, unrolled)
        for p in range(NS):
            unpack_one(c + 1 - div(c + 1, CHUNKS), p)
        weight_grads(c, in2(v), hid_slot)
        if turn:

            @pl.when(c >= 1)
            def _():
                wait_b(v - 1)
                add_b(v - 1, loop)
        sends(v)
        step_a(v)

    def fetch(m):
        return pltpu.make_async_copy(x_in.at[0, rows(m * TL, TL)], xt.at[in2(m)], xt_sem.at[in2(m)])

    def back_through_norm(turn, m):
        part = rows(m * TL, TL)
        by_a = dot(dg[part, :], wg[...], 1, 1) + dot(du[part, :], wu[...], 1, 1)
        by_a = by_a.astype(bf16).astype(f32)
        wide = hx[part, :].astype(f32)
        scale = lax.rsqrt(jnp.mean(wide * wide, -1, keepdims=True) + 1e-6)
        along = jnp.mean(by_a * wide, -1, keepdims=True)
        by_h = (by_a * scale - wide * (scale * scale * scale * along)).astype(bf16)
        by_h = dh[part, :] + by_h
        dh[part, :] = by_h
        return by_h

    loaded()
    unpack(0)
    for copy in fetch_kept(0):
        copy.start()

    def first_1(c):
        backward_half(c, 0)
        pump(CHUNKS + c)
        fence()
        backward_half(c, 1)
        gradients(0, c, 1)

    loop(CHUNKS, first_1)
    load(0)
    fetch(0).start()

    def second_1(m):
        lanes = pl.ds(pl.multiple_of(m * TL, TL), TL)
        fetch(m).wait()
        pl.when(m + 1 < NT)(lambda: fetch(m + 1).start())
        by_h = back_through_norm(0, m)
        dh_t[:, lanes] = by_h.T
        h = xt[in2(m)]
        hx[rows(m * TL, TL), :] = h
        act = normed(h.astype(f32))
        a_t[:, lanes] = act.T
        pl.when(in2(m) == 1)(lambda: tick(CHUNKS + div(m, 2)))

    loop(NT, second_1)

    loaded()
    unpack(0)

    def first_0(c):
        pl.when(c < CHUNKS - 1)(lambda: load(c + 1))
        for copy in fetch_kept(c):
            copy.wait()
        backward_kept(c)

        @pl.when(c < CHUNKS - 1)
        def _():
            for copy in fetch_kept(c + 1):
                copy.start()

        gradients(1, c, mod(c, 2))

    loop(CHUNKS, first_0)

    def second_0(m):
        back_through_norm(1, m)
        part = rows(m * TL, TL)
        pltpu.make_async_copy(dh.at[part], dx_out.at[0, part], io_sem.at[0]).start()
        loop(2, lambda i: pl.when((in2(m) == 1) & (m + i >= 2))(lambda: tick(PERIOD + CHUNKS - 2 + m + i)))

    loop(NT, second_0)

    loop(LG - NT + 1, lambda i: tick(PERIOD + CHUNKS + NT - 1 + i))

    def finish(ch):
        wait(sums.at[ch, pl.ds(0, 3 * QY)], ys_recv.at[ch])
        wait(sums.at[pl.ds(0, 6), pl.ds(0, 688)], g_send.at[ch])

    loop(N, finish)
    wait(got.at[pl.ds(0, CHUNKS), 0, pl.ds(0, 576)], g1_send.at[1])
    wait(dh, io_sem.at[0])


def solution(mesh):
    def step(x, dy, w_gate, w_up, w_down):
        anywhere = pl.BlockSpec(memory_space=pl.ANY)
        shape = jax.ShapeDtypeStruct
        vmem = lambda *dims, dtype=bf16: pltpu.VMEM(dims, dtype)
        dma = lambda *dims: pltpu.SemaphoreType.DMA(dims)
        one = pltpu.SemaphoreType.DMA
        _, _, sums, by_x, _, _ = pl.pallas_call(
            kernel,
            out_shape=(
                shape((N, PART, 128), bf16), shape((N, NS, PART, 128), bf16), shape((N, PADDED, 128), bf16), shape((1, T, D), bf16),
                shape((CHUNKS, 2, T, C), f32), shape((CHUNKS, T, C), bf16),
            ),
            in_specs=[anywhere] * 5,
            out_specs=(anywhere,) * 6,
            scratch_shapes=[
                vmem(T, D), vmem(T, D), vmem(T, D), vmem(D, T), vmem(D, T),
                vmem(D, F), vmem(D, F), vmem(C, D), vmem(2, T, C), vmem(T, F), vmem(T, F), vmem(2, T, C, dtype=f32),
                vmem(NS, PART, 128), vmem(2, TL, D),
                vmem(2, NS, PADDED, 128), vmem(2, NX, PADDED, 128), vmem(2, NX, NY, QY, 128),
                vmem(4, 3, NY, QA, 128), vmem(4, 3, NX, QB, 128),
                vmem(2, 3, QA, 128), vmem(2, 3, QB, 128), vmem(4, 4, QA, 128), vmem(4, 4, QB, 128),
                vmem(4, NZ * QZ, 128), vmem(4, NZ - 1, QZ, 128), vmem(4, NZ * QZ, 128), vmem(2, QY, 128),
                dma(4), one, pltpu.SemaphoreType.REGULAR, dma(2), dma(N), dma(N), dma(N), dma(N), one, dma(2), dma(2), dma(2), one,
                *[dma(4)] * 15, dma(N),
            ],
            compiler_params=pltpu.CompilerParams(collective_id=0, has_side_effects=True, vmem_limit_bytes=67043328),
        )(x, dy, w_gate, w_up, w_down)
        return pl.pallas_call(
            unpack_kernel,
            out_shape=(
                shape((1, T, D), bf16), shape((LAYERS, RG, F), bf16), shape((LAYERS, RG, F), bf16), shape((LAYERS, RD, D), bf16)
            ),
            in_specs=[anywhere] * 2,
            out_specs=(anywhere,) * 4,
            scratch_shapes=[
                vmem(N, PADDED, 128), vmem(T, D), vmem(LAYERS, RG, F), vmem(LAYERS, RG, F), vmem(LAYERS, RD, D),
                dma(2), dma(4), dma(6),
            ],
            compiler_params=pltpu.CompilerParams(vmem_limit_bytes=67043328),
        )(sums, by_x)

    states, cut = P(("rep", "r", "s"), None, None), P(None, "s", None)
    return jax.shard_map(
        step,
        mesh=mesh,
        in_specs=(states, states) + (cut,) * 3,
        out_specs=(states,) + (P("rep", "s", None),) * 3,
        check_vma=False,
    )
```

time: 739 us -> 274 us (0.37)
  waiting for transfers between devices: 365 us -> 0 us
  matrix products: 310 us -> 0 us
  Pallas kernels: 0 us -> 271 us
  local copies, waits for them, and re-layouts: 27.5 us -> 0 us
  other arithmetic: 15.3 us -> 0 us
  between operations: 14.3 us -> 0.8 us
    dot_general x17 -> x0, matrix products: 310 us -> none  [the longest x6 110 us: layer(): up = jnp.dot(a, w['w_up'], preferred_element_type=jnp.float32)]
    pallas_call x0 -> x2, Pallas kernels: none -> 271 us  [the longest x1 263 us: step(): pl.pallas_call(kernel, out_shape=(shape((N, PART, 128), bf16), shape((N,...]
    psum x1 -> x0, waiting for transfers between devices: 141 us -> none  [summed(): lax.psum(lax.psum_scatter(term, 's', scatter_dimension=0, tiled=True), 'r')]
    reduce_scatter x6 -> x0, waiting for transfers between devices: 114 us -> none  [summed(): lax.psum_scatter(term, 's', scatter_dimension=0, tiled=True)]
    all_gather x6 -> x0, waiting for transfers between devices: 109 us -> none  [fetched(): lax.all_gather(w[number], 's', axis=0, tiled=True)]
    unnamed x21 -> x0, local copies, waits for them, and re-layouts: 20.7 us -> none
  transfers between devices with their start and end apart: 13 -> 0, of which waited for: 10 -> 0; matrix products, arithmetic and copies ran while one was open for 36% -> 0% of each run, Pallas kernels for 0% -> 0%
where the time goes in v2:
time: 274 us; the launch traced here: 272 us
  Pallas kernels  271 us (99%)
    pallas_call x1, Pallas kernels, step(): pl.pallas_call(kernel, out_shape=(shape((N, PART, 128), bf16), shape((N,...  263 us
    pallas_call x1, Pallas kernels, step(): pl.pallas_call(unpack_kernel, out_shape=(shape((1, T, D), bf16), shape((L...  7.85 us

profile of v2, /device:TPU:2, one launch (start us, length us, event | category | flops | bytes accessed | tf_op | source)
XLA Modules:
  0.0 272.1 jit_solution(2746070997123702581)
XLA Ops:
  0.6 263.5 %shard_map.84 = (bf16[18,672,128]{2,1,0:T(8,128)(2,1)}, bf16[18,8,672,128]{3,2,1,0:T(8,128)(2,1)}, bf16[18,704,128]{2,1,0:T(8,128)(2,1)}, bf16[1,2048,896]{2,1,0...) custom-call(bf16[1,2048,896]{2,1,0:T(8,128)(2,1)} %x_in.1, bf16[1,2048,896]{2,1,0:T(8,128)(2,1)} %dy_in.1, ...), custom_call_target="tpu_custom_call" | custom-call | tf_op jit(solution)/shard_map/pallas_call | solution.py:620
  264.1 7.8 %shard_map.85 = (bf16[1,2048,896]{2,1,0:T(8,128)(2,1)}, bf16[2,112,2304]{2,1,0:T(8,128)(2,1)}, bf16[2,112,2304]{2,1,0:T(8,128)(2,1)}, bf16[2,288,896]{2,1,0:T(8,128)(2,1)}) custom-call(bf16[18,704,128]{2,1,0:T(8,128)(2,1)} %get-tuple-element.6.sums_in, bf16[1,2048,896]{2,1,0:T(8,128)(2,1)} %get-tuple-element.7.dx_in), custom_call_target="tpu_custom_call" | custom-call | tf_op jit(solution)/shard_map/pallas_call | solution.py:641

commit v3 on v2

--- a/solution.py
+++ b/solution.py
@@ -377,7 +377,7 @@
         for k in range(n):
             body(k)
 
-    def sends(now):
+    def sends(now, steps=steps):
         for lag, _, _, last in steps:
             pl.when(real(now - lag))(lambda: last(now - lag))
 
@@ -392,6 +392,7 @@
     pl.semaphore_wait(barrier, len(peers))
     for ch in range(CHUNKS):
         gather_1(ch, staged(ch), g1_send.at[0])
+    gather_2(0)
     get_x.wait()
 
     def first_norm(m):
@@ -399,7 +400,6 @@
         a[part, :] = normed(hx[part, :].astype(f32))
 
     loop(NT, first_norm)
-    gather_2(0)
     gather_2(1)
     packed()
     pack(1)
@@ -514,6 +514,8 @@
         waits(v, beside)
         pl.when(c < CHUNKS - 1)(loaded)
         adds(v, steps[:-1])
+        sends(v, steps[:-1])
+        fence()
         if not turn:
             add_b(v + 1, unrolled)
         for p in range(NS):
@@ -525,7 +527,7 @@
             def _():
                 wait_b(v - 1)
                 add_b(v - 1, loop)
-        sends(v)
+        sends(v, steps[-1:])
         step_a(v)
 
     def fetch(m):
@@ -569,7 +571,7 @@
         hx[rows(m * TL, TL), :] = h
         act = normed(h.astype(f32))
         a_t[:, lanes] = act.T
-        pl.when(in2(m) == 1)(lambda: tick(CHUNKS + div(m, 2)))
+        pl.when(in2(m) == 0)(lambda: tick(CHUNKS + div(m, 2)))
 
     loop(NT, second_1)
 
@@ -595,7 +597,7 @@
         back_through_norm(1, m)
         part = rows(m * TL, TL)
         pltpu.make_async_copy(dh.at[part], dx_out.at[0, part], io_sem.at[0]).start()
-        loop(2, lambda i: pl.when((in2(m) == 1) & (m + i >= 2))(lambda: tick(PERIOD + CHUNKS - 2 + m + i)))
+        loop(2, lambda i: pl.when((in2(m) == 0) & (m + i >= 1))(lambda: tick(PERIOD + CHUNKS - 1 + m + i)))
 
     loop(NT, second_0)
 

time: 274 us -> 271 us (0.989)
    pallas_call x1, Pallas kernels: 263 us -> 261 us  [step(): pl.pallas_call(kernel, out_shape=(shape((N, PART, 128), bf16), shape((N,...]
where the time goes in v3:
time: 271 us; the launch traced here: 269 us
  Pallas kernels  269 us (99%)
    pallas_call x1, Pallas kernels, step(): pl.pallas_call(kernel, out_shape=(shape((N, PART, 128), bf16), shape((N,...  261 us
    pallas_call x1, Pallas kernels, step(): pl.pallas_call(unpack_kernel, out_shape=(shape((1, T, D), bf16), shape((L...  7.85 us

profile of v3, /device:TPU:2, one launch (start us, length us, event | category | flops | bytes accessed | tf_op | source)
XLA Modules:
  0.0 269.3 jit_solution(11262101746679617477)
XLA Ops:
  0.6 260.7 %shard_map.84 = (bf16[18,672,128]{2,1,0:T(8,128)(2,1)}, bf16[18,8,672,128]{3,2,1,0:T(8,128)(2,1)}, bf16[18,704,128]{2,1,0:T(8,128)(2,1)}, bf16[1,2048,896]{2,1,0...) custom-call(bf16[1,2048,896]{2,1,0:T(8,128)(2,1)} %x_in.1, bf16[1,2048,896]{2,1,0:T(8,128)(2,1)} %dy_in.1, ...), custom_call_target="tpu_custom_call" | custom-call | tf_op jit(solution)/shard_map/pallas_call | solution.py:622
  261.3 7.8 %shard_map.85 = (bf16[1,2048,896]{2,1,0:T(8,128)(2,1)}, bf16[2,112,2304]{2,1,0:T(8,128)(2,1)}, bf16[2,112,2304]{2,1,0:T(8,128)(2,1)}, bf16[2,288,896]{2,1,0:T(8,128)(2,1)}) custom-call(bf16[18,704,128]{2,1,0:T(8,128)(2,1)} %get-tuple-element.6.sums_in, bf16[1,2048,896]{2,1,0:T(8,128)(2,1)} %get-tuple-element.7.dx_in), custom_call_target="tpu_custom_call" | custom-call | tf_op jit(solution)/shard_map/pallas_call | solution.py:643
